TPU v7x, 512 devices: a whole 4x8x8 slice. The times are simulated.
512 devices in a mesh: dp: 8 (over z_hi, core), mp: 64 (over z_lo, x, y).
Axes of the slice: x: 4, y: 8, z: 8 (z_hi: 4, z_lo: 2; z = z_hi * 2 + z_lo), core: 2. Of those that a mesh axis runs over, the one named last changes fastest.
Arguments:
- inputs: bfloat16 [2048, 4096], P('dp'), may hold values from -6 to 6
- upstream: bfloat16 [2048, 4096], P('dp'), may hold values from -6 to 6
- eig_tiles: bfloat16 [64, 8, 2, 128, 128], P('mp'), may hold values from -0.09375 to 0.09375
- eigvals: float32 [4096], replicated, may hold values from 0.25 to 4
Outputs:
- grad_t: bfloat16 [4096, 2048], P('mp', 'dp')
All inputs are finite; a program needn't handle non-finite values.
Results may differ from a plain program's by a relative error of at most 0.013.
Values may be sent and summed in bfloat16 or wider, within the bound.
No kernel may reach another device: no remote copies, remote signals or barrier semaphores. Data moves between devices by JAX's collectives and lax.ppermute only.
A program may use at most 64 MiB of HBM per device.

v0:
```python
import jax
import jax.numpy as jnp
from jax import lax
from jax.sharding import PartitionSpec as P


def split_up(value, dim, length):
    dims = value.shape
    blocks = value.reshape(*dims[:dim], length, dims[dim] // length, *dims[dim + 1 :])
    return jnp.moveaxis(blocks, dim, 0)


def summed_on_arrival(value, axis, dim):
    length = lax.axis_size(axis)
    blocks = lax.all_to_all(split_up(value, dim, length), axis, 0, 0, tiled=True)
    return jnp.sum(blocks.astype(jnp.float32), axis=0)


def laid_out(blocks, dim):
    blocks = jnp.moveaxis(blocks, 0, dim)
    dims = blocks.shape
    return blocks.reshape(*dims[:dim], dims[dim] * dims[dim + 1], *dims[dim + 2 :])


def copy_for_each(value, axis):
    length = lax.axis_size(axis)
    return lax.all_to_all(
        jnp.broadcast_to(value[None], (length, *value.shape)), axis, 0, 0, tiled=True
    )


def gather_directly(value, axis, dim):
    return laid_out(copy_for_each(value, axis), dim)


def kernel_of(left, right):
    root_left = jnp.sqrt(left)[:, None]
    root_right = jnp.sqrt(right)[None, :]
    return -1.0 / (root_left * root_right * (root_left + root_right))


def on_device(inputs, upstream, eig_tiles, eigvals):
    groups = lax.axis_size("mp")
    member = lax.axis_index("mp")
    width = eigvals.shape[0]
    slab = width // groups
    tile_rows = eig_tiles.shape[1]
    tile_cols = eig_tiles.shape[2]
    tile = eig_tiles.shape[3]
    grid_rows = width // (tile_rows * tile)
    grid_cols = groups // grid_rows
    piece = tile_cols * tile // groups
    local = jnp.transpose(eig_tiles[0], (0, 2, 1, 3)).reshape(tile_rows * tile, groups, piece)
    moved = lax.all_to_all(local, "mp", split_axis=1, concat_axis=1, tiled=True)
    moved = moved.reshape(tile_rows, tile, grid_rows, grid_cols, piece)
    basis = jnp.transpose(moved, (0, 2, 1, 3, 4)).reshape(width, slab)
    ordered = jnp.transpose(eigvals.reshape(tile_cols, grid_cols, tile), (1, 0, 2)).reshape(
        grid_cols, groups, piece
    )
    ordered = jnp.transpose(ordered, (1, 0, 2)).reshape(width)
    own = lax.dynamic_slice_in_dim(ordered, member * slab, slab)
    proj_in = jnp.dot(inputs, basis, preferred_element_type=jnp.float32).astype(jnp.bfloat16)
    proj_up = jnp.dot(upstream, basis, preferred_element_type=jnp.float32).astype(jnp.bfloat16)
    stacked = jnp.stack([proj_in, proj_up], 0)
    over_tokens = (((0,), (0,)), ((), ()))
    pieces = lax.all_gather(stacked, "mp", axis=2, tiled=True)
    part_in = pieces[0]
    part_up = pieces[1]
    block = lax.dot_general(proj_in, part_up, over_tokens, preferred_element_type=jnp.float32)
    block = block + lax.dot_general(
        proj_up, part_in, over_tokens, preferred_element_type=jnp.float32
    )
    joined = jnp.concatenate([block, part_in.astype(jnp.float32)], 0)
    gram = joined[:slab]
    all_in = joined[slab:].astype(jnp.bfloat16)
    share = summed_on_arrival(gram.astype(jnp.bfloat16), "dp", 0)
    count = share.shape[0]
    own_part = lax.dynamic_slice_in_dim(own, lax.axis_index("dp") * count, count)
    part = (kernel_of(own_part, ordered) * (0.5 * share)).astype(jnp.bfloat16)
    weighted = gather_directly(part, "dp", 0)
    over_columns = (((1,), (1,)), ((), ()))
    mixed = lax.dot_general(all_in, weighted, over_columns, preferred_element_type=jnp.float32)
    factor = 2.0 / (lax.axis_size("dp") * inputs.shape[0])
    update = (proj_up.astype(jnp.float32) / jnp.sqrt(own)[None, :] + factor * mixed).astype(
        jnp.bfloat16
    )
    own_rows = lax.all_to_all(basis, "mp", split_axis=0, concat_axis=1, tiled=True)
    every_update = gather_directly(update, "mp", 1)
    result = lax.dot_general(
        own_rows, every_update, over_columns, preferred_element_type=jnp.float32
    )
    return result.astype(jnp.bfloat16)


def solution(mesh):
    return jax.shard_map(
        on_device,
        mesh=mesh,
        in_specs=(P("dp", None), P("dp", None), P("mp", None, None, None, None), P()),
        out_specs=P("mp", "dp"),
        check_vma=False,
    )
```

profile of v0, /device:TPU:8, one launch (start us, length us, event | category | flops | bytes accessed | tf_op | source)
XLA Modules:
  0.0 494.4 jit_solution(2258323800576001424)
XLA Ops:
  6.5 0.0 copy-start
  6.5 0.0 all-gather.2.cloned.1.call-start
  6.5 1.5 copy.11
  8.0 0.1 reshape.93
  8.2 30.6 %all_to_all.36 = bf16[1024,64,4]{0,2,1:T(4,128)(2,1)S(1)} all-to-all(bf16[1024,64,4]{0,2,1:T(4,128)(2,1)S(1)} %reshape.93), channel_id=1, replica_groups=mesh['dp'=8,'mp'=64] {'mp'}, dimensions={1} | all-to-all | bytes 1048576 | tf_op jit(solution)/shard_map/all_to_all | solution.py:54
  38.7 1.0 reshape.102
  39.7 1.7 copy.13
  41.4 0.4 reshape.95
  41.8 0.0 copy-done
  41.8 0.0 copy-start.1
  41.8 0.8 convolution_convert_fusion.1
  42.6 0.8 copy-done.1
  43.4 0.8 convolution_convert_fusion
  44.2 0.6 pad_maximum_fusion
  44.8 0.0 all-gather.2.cloned.1.call-update
  44.8 303.2 %all-gather.2.cloned.1.call-done = bf16[2,256,4096]{1,2,0:T(8,128)(2,1)} async-done(((bf16[2,256,64]{1,2,0:T(8,128)(2,1)}), bf16[2,256,4096]{1,2,0:T(8,128)(2,1)}) %all-gather.2.cloned.1.call-update) | async-done | bytes 4194320 | tf_op jit(solution)/shard_map/all_gather | solution.py:66
  348.1 2.3 fusion.2
  350.4 0.0 copy-start.2
  350.4 3.2 fusion.1
  353.6 6.8 %all-to-all-start.1 = ((bf16[8,8,4096]{2,1,0:T(8,128)(2,1)}), bf16[8,8,4096]{2,1,0:T(8,128)(2,1)S(1)}, u32[]{:S(2)}, u32[]{:S(2)}) async-start(bf16[8,8,4096]{2,1,0:T(8,128)(2,1)} %fusion.1), calls=%async_computation.1 | async-start | bytes 1048576 | tf_op jit(solution)/shard_map/all_to_all | solution.py:15
  360.4 0.0 copy-done.2
  360.4 0.1 copy.14
  360.5 1.2 copy.15
  361.8 1.3 reshape.98
  363.1 0.1 dynamic-slice_sqrt_fusion
  363.2 15.2 %all-to-all-done.1 = bf16[8,8,4096]{2,1,0:T(8,128)(2,1)S(1)} async-done(((bf16[8,8,4096]{2,1,0:T(8,128)(2,1)}), bf16[8,8,4096]{2,1,0:T(8,128)(2,1)S(1)}, u32[]{:S(2)}, u32[]{:S(2)}) %all-to-all-start.1) | async-done | bytes 524320 | tf_op jit(solution)/shard_map/all_to_all | solution.py:15
  378.4 0.1 convert_reduce_fusion
  378.5 0.1 multiply_convert_fusion
  378.6 0.9 broadcast_in_dim.4
  379.4 3.5 all-to-all-start.2
  382.9 1.4 all_to_all.28
  384.3 2.9 copy.17
  387.3 3.0 reshape.103
  390.3 10.5 %all-to-all-done.2 = bf16[8,8,4096]{2,1,0:T(8,128)(2,1)S(1)} async-done(((bf16[8,8,4096]{2,1,0:T(8,128)(2,1)}), bf16[8,8,4096]{2,1,0:T(8,128)(2,1)S(1)}, u32[]{:S(2)}, u32[]{:S(2)}) %all-to-all-start.2) | async-done | bytes 524320 | tf_op jit(solution)/shard_map/all_to_all | solution.py:27
  400.8 8.2 %all-to-all-start.4 = ((bf16[64,2,2048]{2,1,0:T(2,128)(2,1)}), bf16[64,2,2048]{2,1,0:T(2,128)(2,1)S(1)}, u32[]{:S(2)}, u32[]{:S(2)}) async-start(bf16[64,2,2048]{2,1,0:T(2,128)(2,1)} %reshape.103), calls=%async_computation.4 | async-start | bytes 1048576 | tf_op jit(solution)/shard_map/all_to_all | solution.py:87
  409.0 0.1 dynamic-slice_sqrt_fusion.1
  409.1 2.1 fusion.11
  411.2 15.7 %all-to-all-done.4 = bf16[64,2,2048]{2,1,0:T(2,128)(2,1)S(1)} async-done(((bf16[64,2,2048]{2,1,0:T(2,128)(2,1)}), bf16[64,2,2048]{2,1,0:T(2,128)(2,1)S(1)}, u32[]{:S(2)}, u32[]{:S(2)}) %all-to-all-start.4) | async-done | bytes 524320 | tf_op jit(solution)/shard_map/all_to_all | solution.py:87
  426.9 1.6 broadcast_in_dim.5
  428.4 5.7 %all-to-all-start.3 = ((bf16[64,256,64]{1,2,0:T(8,128)(2,1)}), bf16[64,256,64]{1,2,0:T(8,128)(2,1)}, u32[]{:S(2)}, u32[]{:S(2)}) async-start(bf16[64,256,64]{1,2,0:T(8,128)(2,1)} %broadcast_in_dim.5), calls=%async_computation.3 | async-start | bytes 4194304 | tf_op jit(solution)/shard_map/all_to_all | solution.py:27
  434.2 1.6 reshape.104
  435.8 48.6 %all-to-all-done.3 = bf16[64,256,64]{1,2,0:T(8,128)(2,1)} async-done(((bf16[64,256,64]{1,2,0:T(8,128)(2,1)}), bf16[64,256,64]{1,2,0:T(8,128)(2,1)}, u32[]{:S(2)}, u32[]{:S(2)}) %all-to-all-start.3) | async-done | bytes 2097184 | tf_op jit(solution)/shard_map/all_to_all | solution.py:27
  484.5 3.0 fusion.15
  (1 shorter events, 0.0 us)
Async XLA Ops:
  6.5 35.3 %copy-start = (bf16[256,4096]{1,0:T(8,128)(2,1)S(1)}, bf16[256,4096]{1,0:T(8,128)(2,1)}, u32[]{:S(2)}) copy-start(bf16[256,4096]{1,0:T(8,128)(2,1)} %param.5) | copy-start | bytes 6291460
  6.5 341.5 %all-gather.2.cloned.1.call-start = ((), (), s32[]{:S(2)}) async-start(), calls=%async_computation.5 | async-start | bytes 4259840 | tf_op jit(solution)/shard_map/all_gather | solution.py:66
  41.8 1.6 copy-start.1
  350.4 10.0 %copy-start.2 = (f32[4096]{0:T(1024)S(1)}, f32[4096]{0:T(1024)}, u32[]{:S(2)}) copy-start(f32[4096]{0:T(1024)} %param.7) | copy-start | bytes 49156
  353.6 24.8 %all-to-all-start.1 = ((bf16[8,8,4096]{2,1,0:T(8,128)(2,1)}), bf16[8,8,4096]{2,1,0:T(8,128)(2,1)S(1)}, u32[]{:S(2)}, u32[]{:S(2)}) async-start(bf16[8,8,4096]{2,1,0:T(8,128)(2,1)} %fusion.1), calls=%async_computation.1 | async-start | bytes 1048576 | tf_op jit(solution)/shard_map/all_to_all | solution.py:15
  379.4 21.4 %all-to-all-start.2 = ((bf16[8,8,4096]{2,1,0:T(8,128)(2,1)}), bf16[8,8,4096]{2,1,0:T(8,128)(2,1)S(1)}, u32[]{:S(2)}, u32[]{:S(2)}) async-start(bf16[8,8,4096]{2,1,0:T(8,128)(2,1)} %broadcast_in_dim.4), calls=%async_computation.2 | async-start | bytes 1048576 | tf_op jit(solution)/shard_map/all_to_all | solution.py:27
  400.8 26.1 %all-to-all-start.4 = ((bf16[64,2,2048]{2,1,0:T(2,128)(2,1)}), bf16[64,2,2048]{2,1,0:T(2,128)(2,1)S(1)}, u32[]{:S(2)}, u32[]{:S(2)}) async-start(bf16[64,2,2048]{2,1,0:T(2,128)(2,1)} %reshape.103), calls=%async_computation.4 | async-start | bytes 1048576 | tf_op jit(solution)/shard_map/all_to_all | solution.py:87
  428.4 56.0 %all-to-all-start.3 = ((bf16[64,256,64]{1,2,0:T(8,128)(2,1)}), bf16[64,256,64]{1,2,0:T(8,128)(2,1)}, u32[]{:S(2)}, u32[]{:S(2)}) async-start(bf16[64,256,64]{1,2,0:T(8,128)(2,1)} %broadcast_in_dim.5), calls=%async_computation.3 | async-start | bytes 4194304 | tf_op jit(solution)/shard_map/all_to_all | solution.py:27
Sparse Core Ops, SparseCore 0:
  45.0 303.0 all-gather.1
where the time goes:
time: 495 us; the launch traced here: 494 us
  waiting for transfers between devices  393 us (79%)
  blocking collectives  30.6 us (6%)
  starting transfers between devices  24.3 us (5%)
  local copies, waits for them, and re-layouts  19.8 us (4%)
  between operations  13.5 us (3%)
  matrix products  12.1 us (2%)
    all_gather x1, waiting for transfers between devices, on_device(): pieces = lax.all_gather(stacked, 'mp', axis=2, tiled=True)  303 us
    all_to_all x2, waiting for transfers between devices, copy_for_each(): lax.all_to_all(jnp.broadcast_to(value[None], (length, *value.shape)), axi...  59.2 us
    all_to_all x1, blocking collectives, on_device(): moved = lax.all_to_all(local, 'mp', split_axis=1, concat_axis=1, tiled=True)  30.6 us
    all_to_all x1, waiting for transfers between devices, on_device(): lax.all_to_all(basis, 'mp', split_axis=0, concat_axis=1, tiled=True)  15.7 us
    all_to_all x1, waiting for transfers between devices, summed_on_arrival(): lax.all_to_all(split_up(value, dim, length), axis, 0, 0, tiled=True)  15.2 us
  transfers between devices with their start and end apart: 5, of which 5 were waited for; matrix products, arithmetic and copies ran while one was open for 3% of the time, Pallas kernels for 0%

commit v1 on v0

--- a/solution.py
+++ b/solution.py
@@ -63,7 +63,9 @@
     proj_up = jnp.dot(upstream, basis, preferred_element_type=jnp.float32).astype(jnp.bfloat16)
     stacked = jnp.stack([proj_in, proj_up], 0)
     over_tokens = (((0,), (0,)), ((), ()))
-    pieces = lax.all_gather(stacked, "mp", axis=2, tiled=True)
+    pieces = jnp.concatenate(
+        lax.all_to_all(jnp.stack([stacked] * lax.axis_size("mp")), "mp", 0, 0), axis=2
+    )
     part_in = pieces[0]
     part_up = pieces[1]
     block = lax.dot_general(proj_in, part_up, over_tokens, preferred_element_type=jnp.float32)

time: 495 us -> 278 us (0.56)
  waiting for transfers between devices: 393 us -> 89.9 us
  blocking collectives: 30.6 us -> 132 us
  between operations: 13.5 us -> 0.15 us
    all_gather x1 -> x0, waiting for transfers between devices: 303 us -> none  [on_device(): pieces = lax.all_gather(stacked, 'mp', axis=2, tiled=True)]
    all_to_all x0 -> x1, blocking collectives: none -> 101 us  [on_device(): lax.all_to_all(jnp.stack([stacked] * lax.axis_size('mp')), 'mp', 0, 0)]
  transfers between devices with their start and end apart: 5 -> 4, of which waited for: 5 -> 4; matrix products, arithmetic and copies ran while one was open for 3% -> 4% of each run, Pallas kernels for 0% -> 0%
where the time goes in v1:
time: 278 us; the launch traced here: 277 us
  blocking collectives  132 us (47%)
  waiting for transfers between devices  89.9 us (32%)
  starting transfers between devices  26.1 us (9%)
  local copies, waits for them, and re-layouts  20.4 us (7%)
  matrix products  8.76 us (3%)
    all_to_all x1, blocking collectives, on_device(): lax.all_to_all(jnp.stack([stacked] * lax.axis_size('mp')), 'mp', 0, 0)  101 us
    all_to_all x2, waiting for transfers between devices, copy_for_each(): lax.all_to_all(jnp.broadcast_to(value[None], (length, *value.shape)), axi...  59 us
    all_to_all x1, blocking collectives, on_device(): moved = lax.all_to_all(local, 'mp', split_axis=1, concat_axis=1, tiled=True)  30.6 us
    all_to_all x1, waiting for transfers between devices, summed_on_arrival(): lax.all_to_all(split_up(value, dim, length), axis, 0, 0, tiled=True)  15.6 us
    all_to_all x1, waiting for transfers between devices, on_device(): lax.all_to_all(basis, 'mp', split_axis=0, concat_axis=1, tiled=True)  15.4 us
    all_to_all x2, starting transfers between devices, copy_for_each(): lax.all_to_all(jnp.broadcast_to(value[None], (length, *value.shape)), axi...  9.88 us
    all_to_all x1, starting transfers between devices, summed_on_arrival(): lax.all_to_all(split_up(value, dim, length), axis, 0, 0, tiled=True)  9.41 us
    all_to_all x1, starting transfers between devices, on_device(): lax.all_to_all(basis, 'mp', split_axis=0, concat_axis=1, tiled=True)  6.85 us
  transfers between devices with their start and end apart: 4, of which 4 were waited for; matrix products, arithmetic and copies ran while one was open for 4% of the time, Pallas kernels for 0%

profile of v1, /device:TPU:8, one launch (start us, length us, event | category | flops | bytes accessed | tf_op | source)
XLA Modules:
  0.0 277.4 jit_solution(18315996536244757299)
XLA Ops:
  0.0 0.0 copy-start
  0.0 1.5 copy.19
  1.5 0.1 reshape.103
  1.6 30.6 %all_to_all.41 = bf16[1024,64,4]{0,2,1:T(4,128)(2,1)S(1)} all-to-all(bf16[1024,64,4]{0,2,1:T(4,128)(2,1)S(1)} %reshape.103), channel_id=1, replica_groups=mesh['dp'=8,'mp'=64] {'mp'}, dimensions={1} | all-to-all | bytes 1048576 | tf_op jit(solution)/shard_map/all_to_all | solution.py:54
  32.2 1.0 reshape.113
  33.2 1.7 copy.21
  34.9 0.4 reshape.105
  35.3 0.0 copy-done
  35.3 0.0 copy-start.3
  35.3 0.8 convolution_convert_fusion.1
  36.1 0.8 copy-done.3
  36.9 0.8 convolution_convert_fusion
  37.7 0.5 stack.11
  38.2 101.3 %all_to_all.42 = bf16[64,2,256,64]{2,3,1,0:T(8,128)(2,1)S(1)} all-to-all(bf16[64,2,256,64]{2,3,1,0:T(8,128)(2,1)S(1)} %stack.11), channel_id=1, replica_groups=mesh['dp'=8,'mp'=64] {'mp'}, dimensions={0} | all-to-all | bytes 8388608 | tf_op jit(solution)/shard_map/all_to_all | solution.py:67
  139.4 0.6 copy.31
  140.0 0.5 fusion.17
  140.6 0.0 copy-start.1
  140.6 0.7 fusion.18
  141.3 0.6 copy-done.1
  141.9 0.0 copy-start.4
  141.9 1.6 fusion.1
  143.5 9.4 %all-to-all-start.2 = ((bf16[8,8,4096]{2,1,0:T(8,128)(2,1)}), bf16[8,8,4096]{2,1,0:T(8,128)(2,1)S(1)}, u32[]{:S(2)}, u32[]{:S(2)}) async-start(bf16[8,8,4096]{2,1,0:T(8,128)(2,1)} %fusion.1), calls=%async_computation.2 | async-start | bytes 1048576 | tf_op jit(solution)/shard_map/all_to_all | solution.py:15
  152.9 0.0 copy-done.4
  152.9 0.1 copy.22
  153.0 1.3 copy.23
  154.2 1.3 reshape.108
  155.6 0.1 dynamic-slice_sqrt_fusion
  155.6 15.6 %all-to-all-done.2 = bf16[8,8,4096]{2,1,0:T(8,128)(2,1)S(1)} async-done(((bf16[8,8,4096]{2,1,0:T(8,128)(2,1)}), bf16[8,8,4096]{2,1,0:T(8,128)(2,1)S(1)}, u32[]{:S(2)}, u32[]{:S(2)}) %all-to-all-start.2) | async-done | bytes 524320 | tf_op jit(solution)/shard_map/all_to_all | solution.py:15
  171.2 0.1 convert_reduce_fusion
  171.3 0.1 multiply_convert_fusion
  171.4 0.8 broadcast_in_dim.4
  172.2 4.1 %all-to-all-start.3 = ((bf16[8,8,4096]{2,1,0:T(8,128)(2,1)}), bf16[8,8,4096]{2,1,0:T(8,128)(2,1)}, u32[]{:S(2)}, u32[]{:S(2)}) async-start(bf16[8,8,4096]{2,1,0:T(8,128)(2,1)} %broadcast_in_dim.4), calls=%async_computation.3 | async-start | bytes 1048576 | tf_op jit(solution)/shard_map/all_to_all | solution.py:27
  176.4 1.4 all_to_all.32
  177.8 2.2 copy.26
  180.0 1.5 reshape.114
  181.5 11.0 %all-to-all-done.3 = bf16[8,8,4096]{2,1,0:T(8,128)(2,1)} async-done(((bf16[8,8,4096]{2,1,0:T(8,128)(2,1)}), bf16[8,8,4096]{2,1,0:T(8,128)(2,1)}, u32[]{:S(2)}, u32[]{:S(2)}) %all-to-all-start.3) | async-done | bytes 524320 | tf_op jit(solution)/shard_map/all_to_all | solution.py:27
  192.6 6.9 %all-to-all-start.5 = ((bf16[64,2,2048]{2,1,0:T(2,128)(2,1)}), bf16[64,2,2048]{2,1,0:T(2,128)(2,1)S(1)}, u32[]{:S(2)}, u32[]{:S(2)}) async-start(bf16[64,2,2048]{2,1,0:T(2,128)(2,1)} %reshape.114), calls=%async_computation.5 | async-start | bytes 1048576 | tf_op jit(solution)/shard_map/all_to_all | solution.py:89
  199.4 0.1 dynamic-slice_sqrt_fusion.1
  199.5 2.2 fusion.8
  201.7 15.4 %all-to-all-done.5 = bf16[64,2,2048]{2,1,0:T(2,128)(2,1)S(1)} async-done(((bf16[64,2,2048]{2,1,0:T(2,128)(2,1)}), bf16[64,2,2048]{2,1,0:T(2,128)(2,1)S(1)}, u32[]{:S(2)}, u32[]{:S(2)}) %all-to-all-start.5) | async-done | bytes 524320 | tf_op jit(solution)/shard_map/all_to_all | solution.py:89
  217.1 0.0 copy-start.2
  217.1 1.6 broadcast_in_dim.5
  218.7 0.0 copy-done.2
  218.7 5.7 %all-to-all-start.4 = ((bf16[64,256,64]{1,2,0:T(8,128)(2,1)}), bf16[64,256,64]{1,2,0:T(8,128)(2,1)}, u32[]{:S(2)}, u32[]{:S(2)}) async-start(bf16[64,256,64]{1,2,0:T(8,128)(2,1)} %broadcast_in_dim.5), calls=%async_computation.4 | async-start | bytes 4194304 | tf_op jit(solution)/shard_map/all_to_all | solution.py:27
  224.4 2.3 reshape.115
  226.7 47.9 %all-to-all-done.4 = bf16[64,256,64]{1,2,0:T(8,128)(2,1)} async-done(((bf16[64,256,64]{1,2,0:T(8,128)(2,1)}), bf16[64,256,64]{1,2,0:T(8,128)(2,1)}, u32[]{:S(2)}, u32[]{:S(2)}) %all-to-all-start.4) | async-done | bytes 2097184 | tf_op jit(solution)/shard_map/all_to_all | solution.py:27
  274.7 2.7 fusion.12
  (2 shorter events, 0.0 us)
Async XLA Ops:
  0.0 35.3 %copy-start = (bf16[256,4096]{1,0:T(8,128)(2,1)S(1)}, bf16[256,4096]{1,0:T(8,128)(2,1)}, u32[]{:S(2)}) copy-start(bf16[256,4096]{1,0:T(8,128)(2,1)} %param.5) | copy-start | bytes 6291460
  35.3 1.6 copy-start.3
  140.6 1.3 copy-start.1
  141.9 11.0 %copy-start.4 = (f32[4096]{0:T(1024)S(1)}, f32[4096]{0:T(1024)}, u32[]{:S(2)}) copy-start(f32[4096]{0:T(1024)} %param.7) | copy-start | bytes 49156
  143.5 27.7 %all-to-all-start.2 = ((bf16[8,8,4096]{2,1,0:T(8,128)(2,1)}), bf16[8,8,4096]{2,1,0:T(8,128)(2,1)S(1)}, u32[]{:S(2)}, u32[]{:S(2)}) async-start(bf16[8,8,4096]{2,1,0:T(8,128)(2,1)} %fusion.1), calls=%async_computation.2 | async-start | bytes 1048576 | tf_op jit(solution)/shard_map/all_to_all | solution.py:15
  172.2 20.3 %all-to-all-start.3 = ((bf16[8,8,4096]{2,1,0:T(8,128)(2,1)}), bf16[8,8,4096]{2,1,0:T(8,128)(2,1)}, u32[]{:S(2)}, u32[]{:S(2)}) async-start(bf16[8,8,4096]{2,1,0:T(8,128)(2,1)} %broadcast_in_dim.4), calls=%async_computation.3 | async-start | bytes 1048576 | tf_op jit(solution)/shard_map/all_to_all | solution.py:27
  192.6 24.6 %all-to-all-start.5 = ((bf16[64,2,2048]{2,1,0:T(2,128)(2,1)}), bf16[64,2,2048]{2,1,0:T(2,128)(2,1)S(1)}, u32[]{:S(2)}, u32[]{:S(2)}) async-start(bf16[64,2,2048]{2,1,0:T(2,128)(2,1)} %reshape.114), calls=%async_computation.5 | async-start | bytes 1048576 | tf_op jit(solution)/shard_map/all_to_all | solution.py:89
  217.1 1.6 copy-start.2
  218.7 56.0 %all-to-all-start.4 = ((bf16[64,256,64]{1,2,0:T(8,128)(2,1)}), bf16[64,256,64]{1,2,0:T(8,128)(2,1)}, u32[]{:S(2)}, u32[]{:S(2)}) async-start(bf16[64,256,64]{1,2,0:T(8,128)(2,1)} %broadcast_in_dim.5), calls=%async_computation.4 | async-start | bytes 4194304 | tf_op jit(solution)/shard_map/all_to_all | solution.py:27
